TPU v7x, 32 devices: a whole 2x2x4 slice. The times are simulated.
32 devices in a mesh: row: 4 (over z), col: 8 (over y, x, core).
Axes of the slice: x: 2, y: 2, z: 4, core: 2. Of those that a mesh axis runs over, the one named last changes fastest.
Arguments:
- grad: float32 [8192, 14336], P(('row', 'col')), may hold values from -30 to 30
- momentum: float32 [8192, 14336], P(('row', 'col')), may hold values from -6 to 6
- weight: float32 [8192, 14336], P(('row', 'col')), may hold values from -0.75 to 0.75
Outputs:
- new_weight: float32 [8192, 14336], P('row', 'col')
- new_momentum: float32 [8192, 14336], P('row', 'col')
All inputs are finite; a program needn't handle non-finite values.
Results may differ from a plain program's by a relative error of at most 0.00002.
Values sent between devices are 32-bit elements; how exact they have to be, the bound alone decides.
A program may use at most 192 MiB of HBM per device.

v0:
```python
import math
import jax
import jax.numpy as jnp
from jax import lax
from jax.sharding import PartitionSpec as P

D = 8192
FF = 14336


def update_state(total, grad, momentum, weight):
    limit = jnp.float32(math.sqrt(D * FF))
    factor = jnp.minimum(jnp.float32(1.0), limit / (jnp.sqrt(total) + jnp.float32(1e-06)))
    new_momentum = jnp.float32(0.9) * momentum + factor * grad
    new_weight = weight - jnp.float32(0.1) * new_momentum
    return (new_weight, new_momentum)


def body(grad, momentum, weight):
    total = lax.psum(jnp.sum(grad * grad), ("row", "col"))
    local_weight, local_momentum = update_state(total, grad, momentum, weight)
    new_weight, new_momentum = (
        lax.all_to_all(local_weight, "col", split_axis=1, concat_axis=0, tiled=True),
        lax.all_to_all(local_momentum, "col", split_axis=1, concat_axis=0, tiled=True),
    )
    return (new_weight, new_momentum)


def solution(mesh):
    in_specs = (P(("row", "col"), None), P(("row", "col"), None), P(("row", "col"), None))
    out_specs = (P("row", "col"), P("row", "col"))
    return jax.shard_map(body, mesh=mesh, in_specs=in_specs, out_specs=out_specs, check_vma=False)
```

profile of v0, /device:TPU:0, one launch (start us, length us, event | category | flops | bytes accessed | tf_op | source)
XLA Modules:
  0.0 447.5 jit_solution(14981939035309159026)
XLA Ops:
  0.6 9.6 %multiply_reduce_fusion = f32[]{:T(128)} fusion(f32[256,14336]{1,0:T(8,128)} %param.3), kind=kLoop, calls=%fused_computation.4 | loop fusion | flops 7340031 | bytes 14680068 | tf_op jit(solution)/shard_map/reduce_sum | solution.py:20
  10.2 42.2 %psum.7 = f32[]{:T(128)} all-reduce(f32[]{:T(128)} %multiply_reduce_fusion), channel_id=1, replica_groups=mesh['row'=4,'col'=8] {'row','col'}, use_global_device_ids=true, to_apply=%region_1.0 | all-reduce | flops 1 | bytes 8 | tf_op jit(solution)/shard_map/psum | solution.py:20
  53.1 25.5 %multiply_subtract_fusion = (f32[256,14336]{1,0:T(8,128)}, f32[256,14336]{1,0:T(8,128)}) fusion(f32[256,14336]{1,0:T(8,128)} %param.5, f32[256,14336]{1,0:T(8,128)} %param.3, f32[]{:T(128)S(6)} %min_shard_map.3, f32[256,14336]{1,0:T(8,128)} %param.4), kind=kLoop, calls=%fused_computation.2 | loop fusion | flops 18350080 | bytes 73400320 | tf_op jit(solution)/shard_map/sub | solution.py:15
  78.6 11.8 %copy.11 = f32[32,8,8,1792]{3,2,0,1:T(8,128)} copy(f32[32,8,8,1792]{3,2,1,0:T(8,128)} %bitcast.17) | data formatting | bytes 29360128 | tf_op jit(solution)/shard_map/all_to_all | solution.py:24
  90.3 5.5 %all-to-all-start.1 = ((f32[256,8,1792]{2,0,1:T(8,128)}), f32[256,8,1792]{2,0,1:T(8,128)}, u32[]{:S(2)}, u32[]{:S(2)}) async-start(f32[256,8,1792]{2,0,1:T(8,128)} %bitcast.15), calls=%async_computation.1 | async-start | bytes 29360128 | tf_op jit(solution)/shard_map/all_to_all | solution.py:24
  95.9 12.0 %copy.12 = f32[32,8,8,1792]{3,2,0,1:T(8,128)} copy(f32[32,8,8,1792]{3,2,1,0:T(8,128)} %bitcast.16) | data formatting | bytes 29360128 | tf_op jit(solution)/shard_map/all_to_all | solution.py:23
  107.9 149.4 %all-to-all-done.1 = f32[256,8,1792]{2,0,1:T(8,128)} async-done(((f32[256,8,1792]{2,0,1:T(8,128)}), f32[256,8,1792]{2,0,1:T(8,128)}, u32[]{:S(2)}, u32[]{:S(2)}) %all-to-all-start.1) | async-done | bytes 14680096 | tf_op jit(solution)/shard_map/all_to_all | solution.py:24
  257.3 5.5 %all-to-all-start = ((f32[256,8,1792]{2,0,1:T(8,128)}), f32[256,8,1792]{2,0,1:T(8,128)}, u32[]{:S(2)}, u32[]{:S(2)}) async-start(f32[256,8,1792]{2,0,1:T(8,128)} %bitcast.14), calls=%async_computation | async-start | bytes 29360128 | tf_op jit(solution)/shard_map/all_to_all | solution.py:23
  262.9 161.5 %all-to-all-done = f32[256,8,1792]{2,0,1:T(8,128)} async-done(((f32[256,8,1792]{2,0,1:T(8,128)}), f32[256,8,1792]{2,0,1:T(8,128)}, u32[]{:S(2)}, u32[]{:S(2)}) %all-to-all-start) | async-done | bytes 14680096 | tf_op jit(solution)/shard_map/all_to_all | solution.py:23
  424.3 11.6 %copy.15 = f32[2048,1792]{1,0:T(8,128)} copy(f32[2048,1792]{1,0:T(8,128)} %bitcast.1) | data formatting | bytes 29360128
  435.9 11.6 %copy.16 = f32[2048,1792]{1,0:T(8,128)} copy(f32[2048,1792]{1,0:T(8,128)} %bitcast.3) | data formatting | bytes 29360128
Async XLA Ops:
  90.3 167.0 %all-to-all-start.1 = ((f32[256,8,1792]{2,0,1:T(8,128)}), f32[256,8,1792]{2,0,1:T(8,128)}, u32[]{:S(2)}, u32[]{:S(2)}) async-start(f32[256,8,1792]{2,0,1:T(8,128)} %bitcast.15), calls=%async_computation.1 | async-start | bytes 29360128 | tf_op jit(solution)/shard_map/all_to_all | solution.py:24
  257.3 167.0 %all-to-all-start = ((f32[256,8,1792]{2,0,1:T(8,128)}), f32[256,8,1792]{2,0,1:T(8,128)}, u32[]{:S(2)}, u32[]{:S(2)}) async-start(f32[256,8,1792]{2,0,1:T(8,128)} %bitcast.14), calls=%async_computation | async-start | bytes 29360128 | tf_op jit(solution)/shard_map/all_to_all | solution.py:23
where the time goes:
time: 448 us; the launch traced here: 447 us
  waiting for transfers between devices  311 us (69%)
  local copies, waits for them, and re-layouts  47 us (10%)
  blocking collectives  42.2 us (9%)
  other arithmetic  35 us (8%)
  starting transfers between devices  11.1 us (2%)
    all_to_all x1, waiting for transfers between devices, body(): lax.all_to_all(local_weight, 'col', split_axis=1, concat_axis=0, tiled=True)  161 us
    all_to_all x1, waiting for transfers between devices, body(): lax.all_to_all(local_momentum, 'col', split_axis=1, concat_axis=0, tiled=...  149 us
    psum x1, blocking collectives, body(): total = lax.psum(jnp.sum(grad * grad), ('row', 'col'))  42.2 us
    sub x1, other arithmetic, update_state(): new_weight = weight - jnp.float32(0.1) * new_momentum  25.5 us
    unnamed x2, local copies, waits for them, and re-layouts  23.2 us
    all_to_all x1, local copies, waits for them, and re-layouts, body(): lax.all_to_all(local_weight, 'col', split_axis=1, concat_axis=0, tiled=True)  12 us
    all_to_all x1, local copies, waits for them, and re-layouts, body(): lax.all_to_all(local_momentum, 'col', split_axis=1, concat_axis=0, tiled=...  11.8 us
    reduce_sum x1, other arithmetic, body(): total = lax.psum(jnp.sum(grad * grad), ('row', 'col'))  9.55 us
  transfers between devices with their start and end apart: 2, of which 2 were waited for; matrix products, arithmetic and copies ran while one was open for 3% of the time, Pallas kernels for 0%

commit v1 on v0

--- a/solution.py
+++ b/solution.py
@@ -1,3 +1,4 @@
+import functools
 import math
 import jax
 import jax.numpy as jnp
@@ -6,6 +7,22 @@
 
 D = 8192
 FF = 14336
+
+
+def run_types(frame_in, axis_tag, ndim_at, array_dim):
+    a_next = jnp.concatenate(
+        lax.all_to_all(
+            jnp.stack(jnp.split(frame_in, lax.axis_size(axis_tag), ndim_at), 0),
+            axis_tag,
+            split_axis=0,
+            concat_axis=0,
+        ),
+        array_dim,
+    )
+    return a_next
+
+
+apply_entries_here = functools.partial(run_types, axis_tag="col", ndim_at=1, array_dim=0)
 
 
 def update_state(total, grad, momentum, weight):
@@ -21,7 +38,7 @@
     local_weight, local_momentum = update_state(total, grad, momentum, weight)
     new_weight, new_momentum = (
         lax.all_to_all(local_weight, "col", split_axis=1, concat_axis=0, tiled=True),
-        lax.all_to_all(local_momentum, "col", split_axis=1, concat_axis=0, tiled=True),
+        apply_entries_here(local_momentum),
     )
     return (new_weight, new_momentum)
 

time: 448 us -> 448 us (level)
  waiting for transfers between devices: 311 us -> 300 us
  local copies, waits for them, and re-layouts: 47 us -> 57.7 us
    all_to_all x1, waiting for transfers between devices: 161 us -> 139 us  [body(): lax.all_to_all(local_weight, 'col', split_axis=1, concat_axis=0, tiled=True)]
    unnamed x2 -> x9, local copies, waits for them, and re-layouts: 23.2 us -> 43.1 us
    all_to_all x1, waiting for transfers between devices: 149 us -> 161 us  [run_types(): lax.all_to_all(jnp.stack(jnp.split(frame_in, lax.axis_size(axis_tag), ndi...]
    all_to_all x1 -> x0, local copies, waits for them, and re-layouts: 11.8 us -> none  [body(): lax.all_to_all(local_momentum, 'col', split_axis=1, concat_axis=0, tiled=...]
  transfers between devices with their start and end apart: 2 -> 2, of which waited for: 2 -> 2; matrix products, arithmetic and copies ran while one was open for 3% -> 5% of each run, Pallas kernels for 0% -> 0%
where the time goes in v1:
time: 448 us; the launch traced here: 447 us
  waiting for transfers between devices  300 us (67%)
  local copies, waits for them, and re-layouts  57.7 us (13%)
  blocking collectives  42.2 us (9%)
  other arithmetic  35 us (8%)
  starting transfers between devices  11.1 us (2%)
    all_to_all x1, waiting for transfers between devices, run_types(): lax.all_to_all(jnp.stack(jnp.split(frame_in, lax.axis_size(axis_tag), ndi...  161 us
    all_to_all x1, waiting for transfers between devices, body(): lax.all_to_all(local_weight, 'col', split_axis=1, concat_axis=0, tiled=True)  139 us
    unnamed x9, local copies, waits for them, and re-layouts  43.1 us
    psum x1, blocking collectives, body(): total = lax.psum(jnp.sum(grad * grad), ('row', 'col'))  42.2 us
    sub x1, other arithmetic, update_state(): new_weight = weight - jnp.float32(0.1) * new_momentum  25.5 us
    all_to_all x1, local copies, waits for them, and re-layouts, body(): lax.all_to_all(local_weight, 'col', split_axis=1, concat_axis=0, tiled=True)  11.8 us
    reduce_sum x1, other arithmetic, body(): total = lax.psum(jnp.sum(grad * grad), ('row', 'col'))  9.55 us
  transfers between devices with their start and end apart: 2, of which 2 were waited for; matrix products, arithmetic and copies ran while one was open for 5% of the time, Pallas kernels for 0%

profile of v1, /device:TPU:0, one launch (start us, length us, event | category | flops | bytes accessed | tf_op | source)
XLA Modules:
  0.0 447.5 jit_solution(17594096824516680522)
XLA Ops:
  0.6 9.6 %multiply_reduce_fusion = f32[]{:T(128)} fusion(f32[256,14336]{1,0:T(8,128)} %param.3), kind=kLoop, calls=%fused_computation.3 | loop fusion | flops 7340031 | bytes 14680068 | tf_op jit(solution)/shard_map/reduce_sum | solution.py:37
  10.2 42.2 %psum.7 = f32[]{:T(128)} all-reduce(f32[]{:T(128)} %multiply_reduce_fusion), channel_id=1, replica_groups=mesh['row'=4,'col'=8] {'row','col'}, use_global_device_ids=true, to_apply=%region_1.0 | all-reduce | flops 1 | bytes 8 | tf_op jit(solution)/shard_map/psum | solution.py:37
  53.1 25.5 %multiply_subtract_fusion = (f32[256,14336]{1,0:T(8,128)}, f32[256,14336]{1,0:T(8,128)}) fusion(f32[256,14336]{1,0:T(8,128)} %param.5, f32[256,14336]{1,0:T(8,128)} %param.3, f32[]{:T(128)S(6)} %min_shard_map.3, f32[256,14336]{1,0:T(8,128)} %param.4), kind=kLoop, calls=%fused_computation.1 | loop fusion | flops 18350080 | bytes 73400320 | tf_op jit(solution)/shard_map/sub | solution.py:32
  78.6 11.8 %copy.8 = f32[32,8,8,1792]{3,2,0,1:T(8,128)} copy(f32[32,8,8,1792]{3,2,1,0:T(8,128)} %bitcast.41) | data formatting | bytes 29360128 | tf_op jit(solution)/shard_map/all_to_all | solution.py:40
  90.3 5.5 %all-to-all-start = ((f32[256,8,1792]{2,0,1:T(8,128)}), f32[256,8,1792]{2,0,1:T(8,128)}, u32[]{:S(2)}, u32[]{:S(2)}) async-start(f32[256,8,1792]{2,0,1:T(8,128)} %bitcast.40), calls=%async_computation | async-start | bytes 29360128 | tf_op jit(solution)/shard_map/all_to_all | solution.py:40
  95.9 2.8 fusion.7
  98.7 2.8 fusion.6
  101.6 2.8 fusion.5
  104.4 2.8 fusion.4
  107.3 2.8 fusion.3
  110.1 2.8 fusion.2
  112.9 2.8 fusion.1
  115.8 2.8 fusion
  118.6 138.7 %all-to-all-done = f32[256,8,1792]{2,0,1:T(8,128)} async-done(((f32[256,8,1792]{2,0,1:T(8,128)}), f32[256,8,1792]{2,0,1:T(8,128)}, u32[]{:S(2)}, u32[]{:S(2)}) %all-to-all-start) | async-done | bytes 14680096 | tf_op jit(solution)/shard_map/all_to_all | solution.py:40
  257.3 5.5 %all-to-all-start.1 = ((f32[8,256,1792]{2,1,0:T(8,128)}), f32[8,256,1792]{2,1,0:T(8,128)}, u32[]{:S(2)}, u32[]{:S(2)}) async-start(f32[8,256,1792]{2,1,0:T(8,128)} %fusion), calls=%async_computation.1 | async-start | bytes 29360128 | tf_op jit(solution)/shard_map/all_to_all | solution.py:14
  262.9 161.5 %all-to-all-done.1 = f32[8,256,1792]{2,1,0:T(8,128)} async-done(((f32[8,256,1792]{2,1,0:T(8,128)}), f32[8,256,1792]{2,1,0:T(8,128)}, u32[]{:S(2)}, u32[]{:S(2)}) %all-to-all-start.1) | async-done | bytes 14680096 | tf_op jit(solution)/shard_map/all_to_all | solution.py:14
  424.3 11.6 %copy.18 = f32[2048,1792]{1,0:T(8,128)} copy(f32[2048,1792]{1,0:T(8,128)} %bitcast.1) | data formatting | bytes 29360128
  435.9 11.6 %copy.19 = f32[2048,1792]{1,0:T(8,128)} copy(f32[2048,1792]{1,0:T(8,128)} %bitcast.10) | data formatting | bytes 29360128
Async XLA Ops:
  90.3 167.0 %all-to-all-start = ((f32[256,8,1792]{2,0,1:T(8,128)}), f32[256,8,1792]{2,0,1:T(8,128)}, u32[]{:S(2)}, u32[]{:S(2)}) async-start(f32[256,8,1792]{2,0,1:T(8,128)} %bitcast.40), calls=%async_computation | async-start | bytes 29360128 | tf_op jit(solution)/shard_map/all_to_all | solution.py:40
  257.3 167.0 %all-to-all-start.1 = ((f32[8,256,1792]{2,1,0:T(8,128)}), f32[8,256,1792]{2,1,0:T(8,128)}, u32[]{:S(2)}, u32[]{:S(2)}) async-start(f32[8,256,1792]{2,1,0:T(8,128)} %fusion), calls=%async_computation.1 | async-start | bytes 29360128 | tf_op jit(solution)/shard_map/all_to_all | solution.py:14
